TPU v7x, 32 devices: a whole 2x2x4 slice. The times are simulated.
32 devices in a mesh: rows: 8 (over z, x), cols: 4 (over y, core).
Axes of the slice: x: 2, y: 2, z: 4, core: 2. Of those that a mesh axis runs over, the one named last changes fastest.
Arguments:
- matrix: float32 [512, 32, 2, 128], P('rows', 'cols'), may hold values from -54 to 54
- plan: int32 [2, 4, 256], replicated, may hold values from 0 to 255, as said below
Outputs:
- rotated: float32 [512, 32, 2, 128], P('rows', 'cols')
Inputs may be any that keep to these rules, and one draw needn't show every extreme that they name: Each plan[s, r] pairs the 256 columns: partner of partner of i is i, and no column is its own partner.
All inputs are finite; a program needn't handle non-finite values.
Results may differ from a plain program's by a relative error of at most 0.0003.
Values sent between devices are 32-bit elements; how exact they have to be, the bound alone decides.
A program may use at most 128 MiB of HBM per device.

v0:
```python
import jax
import jax.numpy as jnp
from jax import lax
from jax.sharding import PartitionSpec as P

STEPS = 2


def passed_along(block, axis, distance):
    devices = range(lax.axis_size(axis))
    route = [((i - distance) % len(devices), i) for i in devices]
    return lax.ppermute(block, axis, route)


def diagonalize(grams, table):
    width = grams.shape[1]
    indices = jnp.arange(width, dtype=jnp.int32)
    rotation = jnp.broadcast_to(jnp.eye(width, dtype=jnp.float32), grams.shape)
    unit_matrix = jnp.eye(width, dtype=jnp.float32)
    for round_index in range(table.shape[0]):
        partner = table[round_index]
        onehot = (partner[:, None] == indices[None, :]).astype(jnp.float32)
        diagonal_now = jnp.diagonal(grams, axis1=1, axis2=2)
        partner_diag = jnp.einsum(
            "pj,ij->pi", diagonal_now, onehot, precision=lax.Precision.HIGHEST
        )
        partner_gram = jnp.sum(grams * onehot[None], axis=2)
        orient = jnp.where(indices < partner, 1.0, -1.0).astype(jnp.float32)
        spread = orient[None, :] * (partner_diag - diagonal_now)
        sign_part = jnp.where(spread >= 0.0, 1.0, -1.0).astype(jnp.float32)
        tangent = (
            sign_part
            * 2.0
            * partner_gram
            / (jnp.abs(spread) + jnp.sqrt(spread * spread + 4.0 * partner_gram * partner_gram))
        )
        cosine = 1.0 / jnp.sqrt(1.0 + tangent * tangent)
        sine_part = tangent * cosine
        off_part = jnp.swapaxes(onehot[None] * (-orient[None, :] * sine_part)[:, :, None], 1, 2)
        rot_now = cosine[:, :, None] * unit_matrix[None] + off_part
        product = jnp.einsum("pij,pjk->pik", grams, rot_now, precision=lax.Precision.HIGHEST)
        grams = jnp.einsum("pji,pjk->pik", rot_now, product, precision=lax.Precision.HIGHEST)
        rotation = jnp.einsum("pij,pjk->pik", rotation, rot_now, precision=lax.Precision.HIGHEST)
    return (grams, rotation)


def full_grams(columns):
    local_sum = jnp.einsum("mpi,mpj->pij", columns, columns, precision=lax.Precision.HIGHEST)
    return lax.psum(local_sum, "rows")


def body(matrix, plan):
    rows_here, pair_here, halves, width = matrix.shape
    columns = matrix.reshape(rows_here, pair_here, halves * width)
    grams = full_grams(columns)
    for step_index in range(STEPS):
        grams, rotation = diagonalize(grams, plan[step_index])
        columns = jnp.einsum("mpi,pij->mpj", columns, rotation, precision=lax.Precision.HIGHEST)
        quarter = columns.reshape(rows_here, pair_here, halves, width)
        tops = quarter[:, :, 0, :]
        bottoms = quarter[:, :, 1, :]
        bottoms, low_grams = passed_along((bottoms, grams[:, width:, width:]), "cols", 1)
        columns = jnp.stack([tops, bottoms], axis=2).reshape(rows_here, pair_here, halves * width)
        if step_index + 1 < STEPS:
            cross_local = jnp.einsum("mpi,mpj->pij", tops, bottoms, precision=lax.Precision.HIGHEST)
            cross = lax.psum(cross_local, "rows")
            upper_rows = jnp.concatenate([grams[:, :width, :width], cross], axis=2)
            lower_rows = jnp.concatenate([jnp.swapaxes(cross, 1, 2), low_grams], axis=2)
            grams = jnp.concatenate([upper_rows, lower_rows], axis=1)
    return columns.reshape(matrix.shape)


def solution(mesh):
    in_specs = (P("rows", "cols", None, None), P())
    out_specs = P("rows", "cols", None, None)
    return jax.shard_map(body, mesh=mesh, in_specs=in_specs, out_specs=out_specs, check_vma=False)
```

profile of v0, /device:TPU:0, one launch (start us, length us, event | category | flops | bytes accessed | tf_op | source)
XLA Modules:
  0.0 463.2 jit_solution(2592383849989567668)
XLA Ops:
  8.0 3.2 fusion.123
  24.4 92.0 %all-reduce.3.cloned.1.call-done = f32[8,256,256]{2,1,0:T(8,128)} async-done(((f32[8,256,256]{2,1,0:T(8,128)}), f32[8,256,256]{2,1,0:T(8,128)}) %all-reduce.3.cloned.1.call-update) | async-done | bytes 2097168 | tf_op jit(solution)/shard_map/psum | solution.py:49
  116.4 17.5 %copy.30 = f32[8,256,256]{0,2,1:T(8,128)} copy(f32[8,256,256]{2,1,0:T(8,128)} %all-reduce.3.cloned.1.call-done) | data formatting | bytes 4194304 | tf_op jit(solution)/shard_map/psum | solution.py:49
  138.7 3.5 fusion.22
  142.2 4.1 fusion.24
  146.3 3.3 multiply_reduce_fusion.6
  149.6 16.5 %copy.32 = f32[8,256,256]{0,2,1:T(8,128)} copy(f32[8,256,256]{1,2,0:T(8,128)S(1)} %get-tuple-element.56) | data formatting | bytes 4194304 | tf_op jit(solution)/shard_map/pji,pjk->pik/dot_general | solution.py:42
  170.1 5.1 %fusion.21 = f32[8,256,256]{1,2,0:T(8,128)S(1)} fusion(f32[8,256,256]{1,2,0:T(8,128)S(1)} %get-tuple-element.56, f32[8,256]{1,0:T(8,128)S(1)} %get-tuple-element.34, f32[256,256]{1,0:T(8,128)} %fusion.135, f32[8,256]{1,0:T(8,128)S(1)} %get-tuple-element.33, f32[256,256]{1,0:T(8,128)S(1)} %get-tuple-element.67), kind=kOutput, calls=%fused_computation.42 | convolution fusion | flops 1612185600 | bytes 4734976 | tf_op jit(solution)/shard_map/pij,pjk->pik/dot_general | solution.py:41
  175.2 3.3 multiply_reduce_fusion.5
  178.6 16.6 %copy.34 = f32[8,256,256]{0,2,1:T(8,128)} copy(f32[8,256,256]{1,2,0:T(8,128)S(1)} %get-tuple-element.58) | data formatting | bytes 4194304 | tf_op jit(solution)/shard_map/pji,pjk->pik/dot_general | solution.py:42
  199.3 5.1 %fusion.18 = f32[8,256,256]{1,2,0:T(8,128)S(1)} fusion(f32[8,256,256]{1,2,0:T(8,128)S(1)} %get-tuple-element.58, f32[8,256]{1,0:T(8,128)S(1)} %get-tuple-element.32, f32[256,256]{1,0:T(8,128)} %fusion.136, f32[8,256]{1,0:T(8,128)S(1)} %get-tuple-element.31, f32[256,256]{1,0:T(8,128)S(1)} %get-tuple-element.67), kind=kOutput, calls=%fused_computation.37 | convolution fusion | flops 1612185600 | bytes 4734976 | tf_op jit(solution)/shard_map/pij,pjk->pik/dot_general | solution.py:41
  204.4 3.3 multiply_reduce_fusion.4
  207.8 16.4 %copy.36 = f32[8,256,256]{0,2,1:T(8,128)} copy(f32[8,256,256]{1,2,0:T(8,128)S(1)} %get-tuple-element.60) | data formatting | bytes 4194304 | tf_op jit(solution)/shard_map/pji,pjk->pik/dot_general | solution.py:42
  228.2 5.1 %fusion.15 = f32[8,256,256]{1,2,0:T(8,128)S(1)} fusion(f32[8,256,256]{1,2,0:T(8,128)S(1)} %get-tuple-element.60, f32[8,256]{1,0:T(8,128)S(1)} %get-tuple-element.30, f32[256,256]{1,0:T(8,128)} %fusion.137, f32[8,256]{1,0:T(8,128)S(1)} %get-tuple-element.29, f32[256,256]{1,0:T(8,128)S(1)} %get-tuple-element.67), kind=kOutput, calls=%fused_computation.32 | convolution fusion | flops 1612185600 | bytes 4734976 | tf_op jit(solution)/shard_map/pij,pjk->pik/dot_general | solution.py:41
  238.5 2.7 fusion.16
  252.7 3.1 collective-permute-done
  259.6 70.2 %all-reduce.5.cloned.1.call-done = f32[8,128,128]{1,2,0:T(8,128)} async-done(((f32[8,128,128]{1,2,0:T(8,128)}), f32[8,128,128]{1,2,0:T(8,128)}) %all-reduce.5.cloned.1.call-update) | async-done | bytes 524304 | tf_op jit(solution)/shard_map/psum | solution.py:66
  333.6 16.7 %copy.43 = f32[8,256,256]{0,2,1:T(8,128)} copy(f32[8,256,256]{1,2,0:T(8,128)S(1)} %get-tuple-element.5) | data formatting | bytes 4194304 | tf_op jit(solution)/shard_map/concatenate | solution.py:69
  353.1 3.5 fusion.12
  356.6 4.1 fusion.11
  360.7 2.7 multiply_reduce_fusion.2
  363.5 16.4 %copy.45 = f32[8,256,256]{0,2,1:T(8,128)} copy(f32[8,256,256]{1,2,0:T(8,128)S(1)} %get-tuple-element.62) | data formatting | bytes 4194304 | tf_op jit(solution)/shard_map/pji,pjk->pik/dot_general | solution.py:42
  382.6 4.1 fusion.8
  386.8 3.8 fusion.9
  390.5 2.7 multiply_reduce_fusion.1
  393.3 16.5 %copy.47 = f32[8,256,256]{0,2,1:T(8,128)} copy(f32[8,256,256]{1,2,0:T(8,128)S(1)} %get-tuple-element.64) | data formatting | bytes 4194304 | tf_op jit(solution)/shard_map/pji,pjk->pik/dot_general | solution.py:42
  412.5 4.1 fusion.5
  416.6 3.8 fusion.6
  420.4 2.7 multiply_reduce_fusion
  423.1 16.5 %copy.49 = f32[8,256,256]{0,2,1:T(8,128)} copy(f32[8,256,256]{1,2,0:T(8,128)S(1)} %get-tuple-element.66) | data formatting | bytes 4194304 | tf_op jit(solution)/shard_map/pji,pjk->pik/dot_general | solution.py:42
  442.3 4.1 fusion
  449.0 5.8 %collective-permute-done.2 = f32[64,8,128]{2,1,0:T(8,128)S(1)} collective-permute-done((f32[64,8,128]{2,1,0:T(8,128)S(1)}, f32[64,8,128]{2,1,0:T(8,128)S(1)}, u32[]{:S(2)}, u32[]{:S(2)}) %collective-permute-start.2) | collective-permute-done | bytes 262176 | tf_op jit(solution)/shard_map/ppermute | solution.py:12
  (172 shorter events, 70.0 us)
Async XLA Ops:
  6.5 109.9 %all-reduce.3.cloned.1.call-start = ((), (), s32[]{:S(2)}) async-start(), calls=%async_computation | async-start | bytes 4194304 | tf_op jit(solution)/shard_map/psum | solution.py:49
  11.2 318.5 %all-reduce.5.cloned.1.call-start = ((), (), s32[]{:S(2)}) async-start(), calls=%async_computation.1 | async-start | bytes 1048576 | tf_op jit(solution)/shard_map/psum | solution.py:66
  11.5 12.9 %copy-start.31 = (s32[1,1,256]{2,1,0:T(1,128)}, s32[1,1,256]{2,1,0:T(1,128)S(1)}, u32[]{:S(2)}) copy-start(s32[1,1,256]{2,1,0:T(1,128)S(1)} %get-tuple-element.22) | copy-start | bytes 3076
  11.5 12.9 %copy-start.33 = (s32[1,1,256]{2,1,0:T(1,128)}, s32[1,1,256]{2,1,0:T(1,128)S(1)}, u32[]{:S(2)}) copy-start(s32[1,1,256]{2,1,0:T(1,128)S(1)} %get-tuple-element.16) | copy-start | bytes 3076
  11.5 12.9 %copy-start.35 = (s32[1,1,256]{2,1,0:T(1,128)}, s32[1,1,256]{2,1,0:T(1,128)S(1)}, u32[]{:S(2)}) copy-start(s32[1,1,256]{2,1,0:T(1,128)S(1)} %get-tuple-element.21) | copy-start | bytes 3076
  11.5 12.9 %copy-start.37 = (s32[1,1,256]{2,1,0:T(1,128)}, s32[1,1,256]{2,1,0:T(1,128)S(1)}, u32[]{:S(2)}) copy-start(s32[1,1,256]{2,1,0:T(1,128)S(1)} %get-tuple-element.20) | copy-start | bytes 3076
  11.5 12.9 %copy-start.38 = (s32[1,1,256]{2,1,0:T(1,128)}, s32[1,1,256]{2,1,0:T(1,128)S(1)}, u32[]{:S(2)}) copy-start(s32[1,1,256]{2,1,0:T(1,128)S(1)} %get-tuple-element.19) | copy-start | bytes 3076
  11.5 12.9 %copy-start.39 = (s32[1,1,256]{2,1,0:T(1,128)}, s32[1,1,256]{2,1,0:T(1,128)S(1)}, u32[]{:S(2)}) copy-start(s32[1,1,256]{2,1,0:T(1,128)S(1)} %get-tuple-element.18) | copy-start | bytes 3076
  11.6 12.9 %copy-start.40 = (s32[1,1,256]{2,1,0:T(1,128)}, s32[1,1,256]{2,1,0:T(1,128)S(1)}, u32[]{:S(2)}) copy-start(s32[1,1,256]{2,1,0:T(1,128)S(1)} %get-tuple-element.17) | copy-start | bytes 3076
  116.4 19.9 %copy-start = (f32[8,256,256]{2,1,0:T(8,128)S(1)}, f32[8,256,256]{2,1,0:T(8,128)}, u32[]{:S(2)}) copy-start(f32[8,256,256]{2,1,0:T(8,128)} %all-reduce.3.cloned.1.call-done) | copy-start | bytes 6291460
  199.2 5.2 %copy-start.27 = (f32[8,256]{1,0:T(8,128)}, f32[8,256]{1,0:T(8,128)S(1)}, u32[]{:S(2)}) copy-start(f32[8,256]{1,0:T(8,128)S(1)} %get-tuple-element.31) | copy-start | bytes 24580
  199.2 5.2 %copy-start.29 = (f32[8,256]{1,0:T(8,128)}, f32[8,256]{1,0:T(8,128)S(1)}, u32[]{:S(2)}) copy-start(f32[8,256]{1,0:T(8,128)S(1)} %get-tuple-element.32) | copy-start | bytes 24580
  199.2 5.2 %copy-start.6 = (f32[256,256]{1,0:T(8,128)S(1)}, f32[256,256]{1,0:T(8,128)}, u32[]{:S(2)}) copy-start(f32[256,256]{1,0:T(8,128)} %fusion.136) | copy-start | bytes 786436
  199.3 5.2 %copy-start.20 = (f32[256,256]{0,1:T(8,128)S(1)}, f32[256,256]{0,1:T(8,128)}, u32[]{:S(2)}) copy-start(f32[256,256]{0,1:T(8,128)} %fusion.129) | copy-start | bytes 786436
  250.0 5.8 %collective-permute-start = (f32[64,8,128]{2,0,1:T(8,128)S(1)}, f32[64,8,128]{2,0,1:T(8,128)S(1)}, u32[]{:S(2)}, u32[]{:S(2)}) collective-permute-start(f32[64,8,128]{2,0,1:T(8,128)S(1)} %bitcast.109), channel_id=1, source_target_pairs={{3,0},{0,1},{1,2},{2,3},{7,4},{4,5},{5,6},{6,7},{11,8},{8,9},{9,10... | collective-permute-start | bytes 786440 | tf_op jit(solution)/shard_map/ppermute | solution.py:12
  251.1 79.9 %collective-permute-start.1 = (f32[8,128,128]{1,2,0:T(8,128)}, f32[8,128,128]{1,2,0:T(8,128)S(1)}, u32[]{:S(2)}, u32[]{:S(2)}) collective-permute-start(f32[8,128,128]{1,2,0:T(8,128)} %get-tuple-element.8), channel_id=1, source_target_pairs={{3,0},{0,1},{1,2},{2,3},{7,4},{4,5},{5,6},{6,7},{11,8},{8,9},{9,10... | collective-permute-start | bytes 1572872 | tf_op jit(solution)/shard_map/ppermute | solution.py:12
  333.6 19.2 %copy-start.36 = (s32[1,1,256]{2,1,0:T(1,128)S(1)}, s32[1,1,256]{2,1,0:T(1,128)}, u32[]{:S(2)}) copy-start(s32[1,1,256]{2,1,0:T(1,128)} %copy-done.35) | copy-start | bytes 3076
  333.6 19.2 %copy-start.46 = (f32[256]{0:T(256)S(1)}, f32[256]{0:T(256)}, u32[]{:S(2)}) copy-start(f32[256]{0:T(256)} %get-tuple-element.43) | copy-start | bytes 3076
  333.6 19.2 %copy-start.47 = (f32[256]{0:T(256)S(1)}, f32[256]{0:T(256)}, u32[]{:S(2)}) copy-start(f32[256]{0:T(256)} %get-tuple-element.44) | copy-start | bytes 3076
  333.6 19.5 %copy-start.10 = (f32[256,256]{1,0:T(8,128)S(1)}, f32[256,256]{1,0:T(8,128)}, u32[]{:S(2)}) copy-start(f32[256,256]{1,0:T(8,128)} %fusion.138) | copy-start | bytes 786436
  350.3 6.2 %copy-start.11 = (f32[8,128,128]{1,2,0:T(8,128)S(1)}, f32[8,128,128]{1,2,0:T(8,128)}, u32[]{:S(2)}) copy-start(f32[8,128,128]{1,2,0:T(8,128)} %all-reduce.5.cloned.1.call-done) | copy-start | bytes 1572868
  350.3 6.2 %copy-start.13 = (f32[8,128,128]{1,2,0:T(8,128)S(1)}, f32[8,128,128]{1,2,0:T(8,128)}, u32[]{:S(2)}) copy-start(f32[8,128,128]{1,2,0:T(8,128)} %copy-done.12) | copy-start | bytes 1572868
  350.3 6.2 %copy-start.14 = (f32[8,128,128]{1,2,0:T(8,128)S(1)}, f32[8,128,128]{1,2,0:T(8,128)}, u32[]{:S(2)}) copy-start(f32[8,128,128]{1,2,0:T(8,128)} %get-tuple-element.7) | copy-start | bytes 1572868
  350.3 6.2 %copy-start.24 = (f32[8,128,128]{1,2,0:T(8,128)S(1)}, f32[8,128,128]{1,2,0:T(8,128)}, u32[]{:S(2)}) copy-start(f32[8,128,128]{1,2,0:T(8,128)} %copy-done.23) | copy-start | bytes 1572868
  363.5 18.9 %copy-start.34 = (s32[1,1,256]{2,1,0:T(1,128)S(1)}, s32[1,1,256]{2,1,0:T(1,128)}, u32[]{:S(2)}) copy-start(s32[1,1,256]{2,1,0:T(1,128)} %copy-done.33) | copy-start | bytes 3076
  363.5 18.9 %copy-start.44 = (f32[256]{0:T(256)S(1)}, f32[256]{0:T(256)}, u32[]{:S(2)}) copy-start(f32[256]{0:T(256)} %get-tuple-element.41) | copy-start | bytes 3076
  363.5 18.8 %copy-start.45 = (f32[256]{0:T(256)S(1)}, f32[256]{0:T(256)}, u32[]{:S(2)}) copy-start(f32[256]{0:T(256)} %get-tuple-element.42) | copy-start | bytes 3076
  393.3 18.9 %copy-start.32 = (s32[1,1,256]{2,1,0:T(1,128)S(1)}, s32[1,1,256]{2,1,0:T(1,128)}, u32[]{:S(2)}) copy-start(s32[1,1,256]{2,1,0:T(1,128)} %copy-done.31) | copy-start | bytes 3076
  393.3 18.9 %copy-start.42 = (f32[256]{0:T(256)S(1)}, f32[256]{0:T(256)}, u32[]{:S(2)}) copy-start(f32[256]{0:T(256)} %get-tuple-element.39) | copy-start | bytes 3076
  393.3 18.9 %copy-start.43 = (f32[256]{0:T(256)S(1)}, f32[256]{0:T(256)}, u32[]{:S(2)}) copy-start(f32[256]{0:T(256)} %get-tuple-element.40) | copy-start | bytes 3076
  423.1 19.2 %copy-start.19 = (f32[256,256]{1,0:T(8,128)S(1)}, f32[256,256]{1,0:T(8,128)}, u32[]{:S(2)}) copy-start(f32[256,256]{1,0:T(8,128)} %fusion.141) | copy-start | bytes 786436
  449.0 5.8 %collective-permute-start.2 = (f32[64,8,128]{2,1,0:T(8,128)S(1)}, f32[64,8,128]{2,1,0:T(8,128)S(1)}, u32[]{:S(2)}, u32[]{:S(2)}) collective-permute-start(f32[64,8,128]{2,1,0:T(8,128)S(1)} %bitcast.108), channel_id=1, source_target_pairs={{3,0},{0,1},{1,2},{2,3},{7,4},{4,5},{5,6},{6,7},{11,8},{8,9},{9,10... | collective-permute-start | bytes 786440 | tf_op jit(solution)/shard_map/ppermute | solution.py:12
  (21 other events, 73.5 us)
Sparse Core Ops, SparseCore 0:
  11.4 105.0 all-reduce.2
  257.8 71.9 all-reduce.4
where the time goes:
time: 467 us; the launch traced here: 463 us
  waiting for transfers between devices  171 us (37%)
  local copies, waits for them, and re-layouts  165 us (35%)
  matrix products  92.9 us (20%)
  other arithmetic  18 us (4%)
  between operations  14.6 us (3%)
    dot_general x6, local copies, waits for them, and re-layouts, diagonalize(): jnp.einsum('pji,pjk->pik', rot_now, product, precision=lax.Precision.HIGH...  98.9 us
    psum x1, waiting for transfers between devices, full_grams(): return lax.psum(local_sum, 'rows')  92 us
    psum x1, waiting for transfers between devices, body(): cross = lax.psum(cross_local, 'rows')  70.2 us
    dot_general x7, matrix products, diagonalize(): jnp.einsum('pij,pjk->pik', grams, rot_now, precision=lax.Precision.HIGHEST)  31.7 us
    dot_general x8, matrix products, diagonalize(): jnp.einsum('pij,pjk->pik', rotation, rot_now, precision=lax.Precision.HIG...  26.3 us
    gather x16, local copies, waits for them, and re-layouts, diagonalize(): diagonal_now = jnp.diagonal(grams, axis1=1, axis2=2)  21 us
    dot_general x7, matrix products, diagonalize(): jnp.einsum('pji,pjk->pik', rot_now, product, precision=lax.Precision.HIGH...  20.8 us
    psum x1, local copies, waits for them, and re-layouts, full_grams(): return lax.psum(local_sum, 'rows')  17.5 us
  transfers between devices with their start and end apart: 5, of which 4 were waited for; matrix products, arithmetic and copies ran while one was open for 4% of the time, Pallas kernels for 0%

commit v1 on v0

--- a/solution.py
+++ b/solution.py
@@ -46,7 +46,7 @@
 
 def full_grams(columns):
     local_sum = jnp.einsum("mpi,mpj->pij", columns, columns, precision=lax.Precision.HIGHEST)
-    return lax.psum(local_sum, "rows")
+    return jnp.sum(lax.all_gather(local_sum, "rows"), axis=0)
 
 
 def body(matrix, plan):

time: 467 us -> 601 us (1.29)
  waiting for transfers between devices: 171 us -> 295 us
  other arithmetic: 18 us -> 25.2 us
    all_gather x0 -> x1, waiting for transfers between devices: none -> 217 us  [full_grams(): return jnp.sum(lax.all_gather(local_sum, 'rows'), axis=0)]
    psum x1 -> x0, waiting for transfers between devices: 92 us -> none  [full_grams(): return lax.psum(local_sum, 'rows')]
    psum x1 -> x0, local copies, waits for them, and re-layouts: 17.5 us -> none  [full_grams(): return lax.psum(local_sum, 'rows')]
    reduce_sum x0 -> x1, local copies, waits for them, and re-layouts: none -> 16.8 us  [full_grams(): return jnp.sum(lax.all_gather(local_sum, 'rows'), axis=0)]
    reduce_sum x0 -> x1, other arithmetic: none -> 7.24 us  [full_grams(): return jnp.sum(lax.all_gather(local_sum, 'rows'), axis=0)]
  transfers between devices with their start and end apart: 5 -> 5, of which waited for: 4 -> 4; matrix products, arithmetic and copies ran while one was open for 4% -> 3% of each run, Pallas kernels for 0% -> 0%
where the time goes in v1:
time: 601 us; the launch traced here: 596 us
  waiting for transfers between devices  295 us (49%)
  local copies, waits for them, and re-layouts  165 us (27%)
  matrix products  94 us (16%)
  other arithmetic  25.2 us (4%)
  between operations  14.7 us (2%)
    all_gather x1, waiting for transfers between devices, full_grams(): return jnp.sum(lax.all_gather(local_sum, 'rows'), axis=0)  217 us
    dot_general x6, local copies, waits for them, and re-layouts, diagonalize(): jnp.einsum('pji,pjk->pik', rot_now, product, precision=lax.Precision.HIGH...  99.8 us
    psum x1, waiting for transfers between devices, body(): cross = lax.psum(cross_local, 'rows')  69.1 us
    dot_general x7, matrix products, diagonalize(): jnp.einsum('pij,pjk->pik', grams, rot_now, precision=lax.Precision.HIGHEST)  32.7 us
    dot_general x8, matrix products, diagonalize(): jnp.einsum('pij,pjk->pik', rotation, rot_now, precision=lax.Precision.HIG...  26.3 us
    gather x16, local copies, waits for them, and re-layouts, diagonalize(): diagonal_now = jnp.diagonal(grams, axis1=1, axis2=2)  21.5 us
    dot_general x7, matrix products, diagonalize(): jnp.einsum('pji,pjk->pik', rot_now, product, precision=lax.Precision.HIGH...  20.8 us
    concatenate x1, local copies, waits for them, and re-layouts, body(): grams = jnp.concatenate([upper_rows, lower_rows], axis=1)  16.8 us
  transfers between devices with their start and end apart: 5, of which 4 were waited for; matrix products, arithmetic and copies ran while one was open for 3% of the time, Pallas kernels for 0%

profile of v1, /device:TPU:0, one launch (start us, length us, event | category | flops | bytes accessed | tf_op | source)
XLA Modules:
  0.0 596.1 jit_solution(5183554303513472831)
XLA Ops:
  8.0 3.2 fusion.123
  24.3 217.1 %all-gather.3.cloned.1.call-done = f32[64,256,256]{2,1,0:T(8,128)} async-done(((f32[8,256,256]{2,1,0:T(8,128)}), f32[64,256,256]{2,1,0:T(8,128)}) %all-gather.3.cloned.1.call-update) | async-done | bytes 16777232 | tf_op jit(solution)/shard_map/all_gather | solution.py:49
  241.4 7.2 %reduce_sum.81 = f32[8,256,256]{2,1,0:T(8,128)S(1)} reduce(f32[8,8,256,256]{3,2,1,0:T(8,128)} %bitcast.104, f32[]{:T(128)} %constant.28.clone.1), dimensions={0}, to_apply=%region_0.0 | reduce | flops 3670016 | bytes 18874372 | tf_op jit(solution)/shard_map/reduce_sum | solution.py:49
  248.6 16.8 %copy.55 = f32[8,256,256]{0,2,1:T(8,128)} copy(f32[8,256,256]{2,1,0:T(8,128)S(1)} %reduce_sum.81) | data formatting | bytes 4194304 | tf_op jit(solution)/shard_map/reduce_sum | solution.py:49
  270.8 5.0 fusion.24
  275.8 3.5 fusion.22
  279.3 3.3 multiply_reduce_fusion.6
  282.7 16.6 %copy.62 = f32[8,256,256]{0,2,1:T(8,128)} copy(f32[8,256,256]{1,2,0:T(8,128)S(1)} %get-tuple-element.56) | data formatting | bytes 4194304 | tf_op jit(solution)/shard_map/pji,pjk->pik/dot_general | solution.py:42
  303.3 5.1 fusion.21
  308.4 3.3 multiply_reduce_fusion.5
  311.8 16.8 %copy.66 = f32[8,256,256]{0,2,1:T(8,128)} copy(f32[8,256,256]{1,2,0:T(8,128)S(1)} %get-tuple-element.58) | data formatting | bytes 4194304 | tf_op jit(solution)/shard_map/pji,pjk->pik/dot_general | solution.py:42
  332.6 5.1 fusion.18
  337.7 3.3 multiply_reduce_fusion.4
  341.1 16.6 %copy.70 = f32[8,256,256]{0,2,1:T(8,128)} copy(f32[8,256,256]{1,2,0:T(8,128)S(1)} %get-tuple-element.60) | data formatting | bytes 4194304 | tf_op jit(solution)/shard_map/pji,pjk->pik/dot_general | solution.py:42
  361.6 5.1 fusion.15
  372.0 2.7 fusion.16
  386.2 3.1 collective-permute-done
  393.0 69.1 %all-reduce.2.cloned.1.call-done = f32[8,128,128]{1,2,0:T(8,128)} async-done(((f32[8,128,128]{1,2,0:T(8,128)}), f32[8,128,128]{1,2,0:T(8,128)}) %all-reduce.2.cloned.1.call-update) | async-done | bytes 524304 | tf_op jit(solution)/shard_map/psum | solution.py:66
  466.0 16.8 %copy.79 = f32[8,256,256]{0,2,1:T(8,128)} copy(f32[8,256,256]{1,2,0:T(8,128)S(1)} %get-tuple-element.5) | data formatting | bytes 4194304 | tf_op jit(solution)/shard_map/concatenate | solution.py:69
  485.6 3.5 fusion.12
  489.1 4.1 fusion.11
  493.2 2.7 multiply_reduce_fusion.2
  496.0 16.6 %copy.83 = f32[8,256,256]{0,2,1:T(8,128)} copy(f32[8,256,256]{1,2,0:T(8,128)S(1)} %get-tuple-element.62) | data formatting | bytes 4194304 | tf_op jit(solution)/shard_map/pji,pjk->pik/dot_general | solution.py:42
  515.3 4.1 fusion.8
  519.4 3.8 fusion.9
  526.0 16.6 %copy.87 = f32[8,256,256]{0,2,1:T(8,128)} copy(f32[8,256,256]{1,2,0:T(8,128)S(1)} %get-tuple-element.64) | data formatting | bytes 4194304 | tf_op jit(solution)/shard_map/pji,pjk->pik/dot_general | solution.py:42
  545.3 4.1 fusion.5
  549.4 3.8 fusion.6
  553.2 2.7 multiply_reduce_fusion
  555.9 16.7 %copy.91 = f32[8,256,256]{0,2,1:T(8,128)} copy(f32[8,256,256]{1,2,0:T(8,128)S(1)} %get-tuple-element.66) | data formatting | bytes 4194304 | tf_op jit(solution)/shard_map/pji,pjk->pik/dot_general | solution.py:42
  575.3 4.1 fusion
  582.0 5.8 collective-permute-done.2
  (171 shorter events, 73.1 us)
Async XLA Ops:
  6.5 234.9 %all-gather.3.cloned.1.call-start = ((), (), s32[]{:S(2)}) async-start(), calls=%async_computation.1 | async-start | bytes 18874368 | tf_op jit(solution)/shard_map/all_gather | solution.py:49
  11.2 450.9 %all-reduce.2.cloned.1.call-start = ((), (), s32[]{:S(2)}) async-start(), calls=%async_computation | async-start | bytes 1048576 | tf_op jit(solution)/shard_map/psum | solution.py:66
  11.3 12.9 %copy-start.30 = (s32[1,1,256]{2,1,0:T(1,128)}, s32[1,1,256]{2,1,0:T(1,128)S(1)}, u32[]{:S(2)}) copy-start(s32[1,1,256]{2,1,0:T(1,128)S(1)} %get-tuple-element.22) | copy-start | bytes 3076
  11.3 12.9 %copy-start.32 = (s32[1,1,256]{2,1,0:T(1,128)}, s32[1,1,256]{2,1,0:T(1,128)S(1)}, u32[]{:S(2)}) copy-start(s32[1,1,256]{2,1,0:T(1,128)S(1)} %get-tuple-element.16) | copy-start | bytes 3076
  11.4 12.9 %copy-start.34 = (s32[1,1,256]{2,1,0:T(1,128)}, s32[1,1,256]{2,1,0:T(1,128)S(1)}, u32[]{:S(2)}) copy-start(s32[1,1,256]{2,1,0:T(1,128)S(1)} %get-tuple-element.21) | copy-start | bytes 3076
  11.4 12.9 %copy-start.36 = (s32[1,1,256]{2,1,0:T(1,128)}, s32[1,1,256]{2,1,0:T(1,128)S(1)}, u32[]{:S(2)}) copy-start(s32[1,1,256]{2,1,0:T(1,128)S(1)} %get-tuple-element.20) | copy-start | bytes 3076
  11.4 12.9 %copy-start.37 = (s32[1,1,256]{2,1,0:T(1,128)}, s32[1,1,256]{2,1,0:T(1,128)S(1)}, u32[]{:S(2)}) copy-start(s32[1,1,256]{2,1,0:T(1,128)S(1)} %get-tuple-element.19) | copy-start | bytes 3076
  11.4 12.9 %copy-start.38 = (s32[1,1,256]{2,1,0:T(1,128)}, s32[1,1,256]{2,1,0:T(1,128)S(1)}, u32[]{:S(2)}) copy-start(s32[1,1,256]{2,1,0:T(1,128)S(1)} %get-tuple-element.18) | copy-start | bytes 3076
  11.4 12.9 %copy-start.39 = (s32[1,1,256]{2,1,0:T(1,128)}, s32[1,1,256]{2,1,0:T(1,128)S(1)}, u32[]{:S(2)}) copy-start(s32[1,1,256]{2,1,0:T(1,128)S(1)} %get-tuple-element.17) | copy-start | bytes 3076
  303.3 5.1 copy-start.24
  332.5 5.2 copy-start.26
  332.6 5.2 copy-start.28
  332.6 5.2 copy-start.4
  332.6 5.2 copy-start.19
  383.5 5.8 collective-permute-start
  384.6 78.8 %collective-permute-start.1 = (f32[8,128,128]{1,2,0:T(8,128)}, f32[8,128,128]{1,2,0:T(8,128)S(1)}, u32[]{:S(2)}, u32[]{:S(2)}) collective-permute-start(f32[8,128,128]{1,2,0:T(8,128)} %get-tuple-element.8), channel_id=1, source_target_pairs={{3,0},{0,1},{1,2},{2,3},{7,4},{4,5},{5,6},{6,7},{11,8},{8,9},{9,10... | collective-permute-start | bytes 1572872 | tf_op jit(solution)/shard_map/ppermute | solution.py:12
  466.0 19.3 %copy-start.35 = (s32[1,1,256]{2,1,0:T(1,128)S(1)}, s32[1,1,256]{2,1,0:T(1,128)}, u32[]{:S(2)}) copy-start(s32[1,1,256]{2,1,0:T(1,128)} %copy-done.34) | copy-start | bytes 3076
  466.0 19.3 %copy-start.45 = (f32[256]{0:T(256)S(1)}, f32[256]{0:T(256)}, u32[]{:S(2)}) copy-start(f32[256]{0:T(256)} %get-tuple-element.43) | copy-start | bytes 3076
  466.0 19.3 %copy-start.46 = (f32[256]{0:T(256)S(1)}, f32[256]{0:T(256)}, u32[]{:S(2)}) copy-start(f32[256]{0:T(256)} %get-tuple-element.44) | copy-start | bytes 3076
  466.0 19.6 %copy-start.9 = (f32[256,256]{1,0:T(8,128)S(1)}, f32[256,256]{1,0:T(8,128)}, u32[]{:S(2)}) copy-start(f32[256,256]{1,0:T(8,128)} %fusion.138) | copy-start | bytes 786436
  482.9 6.2 %copy-start.10 = (f32[8,128,128]{1,2,0:T(8,128)S(1)}, f32[8,128,128]{1,2,0:T(8,128)}, u32[]{:S(2)}) copy-start(f32[8,128,128]{1,2,0:T(8,128)} %all-reduce.2.cloned.1.call-done) | copy-start | bytes 1572868
  482.9 6.2 %copy-start.12 = (f32[8,128,128]{1,2,0:T(8,128)S(1)}, f32[8,128,128]{1,2,0:T(8,128)}, u32[]{:S(2)}) copy-start(f32[8,128,128]{1,2,0:T(8,128)} %copy-done.11) | copy-start | bytes 1572868
  482.9 6.2 %copy-start.13 = (f32[8,128,128]{1,2,0:T(8,128)S(1)}, f32[8,128,128]{1,2,0:T(8,128)}, u32[]{:S(2)}) copy-start(f32[8,128,128]{1,2,0:T(8,128)} %get-tuple-element.7) | copy-start | bytes 1572868
  482.9 6.2 %copy-start.23 = (f32[8,128,128]{1,2,0:T(8,128)S(1)}, f32[8,128,128]{1,2,0:T(8,128)}, u32[]{:S(2)}) copy-start(f32[8,128,128]{1,2,0:T(8,128)} %copy-done.22) | copy-start | bytes 1572868
  496.0 19.0 %copy-start.33 = (s32[1,1,256]{2,1,0:T(1,128)S(1)}, s32[1,1,256]{2,1,0:T(1,128)}, u32[]{:S(2)}) copy-start(s32[1,1,256]{2,1,0:T(1,128)} %copy-done.32) | copy-start | bytes 3076
  496.0 19.0 %copy-start.43 = (f32[256]{0:T(256)S(1)}, f32[256]{0:T(256)}, u32[]{:S(2)}) copy-start(f32[256]{0:T(256)} %get-tuple-element.41) | copy-start | bytes 3076
  496.0 19.0 %copy-start.44 = (f32[256]{0:T(256)S(1)}, f32[256]{0:T(256)}, u32[]{:S(2)}) copy-start(f32[256]{0:T(256)} %get-tuple-element.42) | copy-start | bytes 3076
  525.9 19.0 %copy-start.31 = (s32[1,1,256]{2,1,0:T(1,128)S(1)}, s32[1,1,256]{2,1,0:T(1,128)}, u32[]{:S(2)}) copy-start(s32[1,1,256]{2,1,0:T(1,128)} %copy-done.30) | copy-start | bytes 3076
  525.9 19.0 %copy-start.41 = (f32[256]{0:T(256)S(1)}, f32[256]{0:T(256)}, u32[]{:S(2)}) copy-start(f32[256]{0:T(256)} %get-tuple-element.39) | copy-start | bytes 3076
  526.0 19.0 %copy-start.42 = (f32[256]{0:T(256)S(1)}, f32[256]{0:T(256)}, u32[]{:S(2)}) copy-start(f32[256]{0:T(256)} %get-tuple-element.40) | copy-start | bytes 3076
  555.9 19.4 %copy-start.18 = (f32[256,256]{1,0:T(8,128)S(1)}, f32[256,256]{1,0:T(8,128)}, u32[]{:S(2)}) copy-start(f32[256,256]{1,0:T(8,128)} %fusion.141) | copy-start | bytes 786436
  581.9 5.8 collective-permute-start.2
  (20 other events, 70.3 us)
Sparse Core Ops, SparseCore 0:
  11.4 229.9 all-gather.2
  391.3 70.8 all-reduce.1
